TPU v7x, 32 devices: a whole 2x2x4 slice. The times are simulated.
32 devices in a mesh: dp: 4 (over y, core), mp: 8 (over z, x).
Axes of the slice: x: 2, y: 2, z: 4, core: 2. Of those that a mesh axis runs over, the one named last changes fastest.
Arguments:
- emb_grad: float32 [65536, 7168], P('dp', 'mp'), may hold values from -600 to 600
- mtp_grad: float32 [14336, 7168], P('dp', 'mp'), may hold values from -600 to 600
- emb_groups: int32 [64], replicated, may hold values from 0 to 31
- mtp_groups: int32 [32], replicated, may hold values from 0 to 31
- max_rms: float32 [1], replicated, may hold values from 0.5 to 2
Outputs:
- emb_clipped: bfloat16 [65536, 7168], P(('dp', 'mp'))
- mtp_clipped: bfloat16 [14336, 7168], P('dp', 'mp')
- group_rms: float32 [32], replicated
All inputs are finite; a program needn't handle non-finite values.
Results may differ from a plain program's by a relative error of at most 0.005.
Values may be sent and summed in bfloat16 or wider, within the bound.
A program may use at most 192 MiB of HBM per device.

v0:
```python
import jax
import jax.numpy as jnp
from jax import lax
from jax.sharding import PartitionSpec as P

D = 7168
V = 65536
CAT = 14336
EMB_BLK = 1024
MTP_BLK = 448
GROUPS = 32


def block_squares(gradient, block_rows):
    blocks = gradient.reshape(gradient.shape[0] // block_rows, block_rows, gradient.shape[1])
    return jnp.sum(jnp.square(blocks), axis=(1, 2))


def membership(labels):
    return (labels[:, None] == jnp.arange(GROUPS, dtype=jnp.int32)[None, :]).astype(jnp.float32)


def on_device(emb_grad, mtp_grad, emb_groups, mtp_groups, max_rms):
    shard = lax.axis_index("dp")
    embed_count = emb_grad.shape[0] // EMB_BLK
    head_count = mtp_grad.shape[0] // MTP_BLK
    embed_labels = lax.dynamic_slice_in_dim(emb_groups, shard * embed_count, embed_count)
    head_labels = lax.dynamic_slice_in_dim(mtp_groups, shard * head_count, head_count)
    emb_low = lax.optimization_barrier(emb_grad.astype(jnp.bfloat16))
    arrived = lax.all_to_all(emb_low, "mp", split_axis=0, concat_axis=1, tiled=True)
    partial_value = jnp.sum(
        block_squares(emb_grad, EMB_BLK)[:, None] * membership(embed_labels), axis=0
    )
    partial_value = partial_value + jnp.sum(
        block_squares(mtp_grad, MTP_BLK)[:, None] * membership(head_labels), axis=0
    )
    group_square = lax.psum(partial_value, ("dp", "mp"))
    group_size = jnp.sum(membership(emb_groups), axis=0) * jnp.float32(EMB_BLK * D) + jnp.sum(
        membership(mtp_groups), axis=0
    ) * jnp.float32(MTP_BLK * D)
    group_rms = jnp.sqrt(group_square / jnp.maximum(group_size, 1.0))
    global_norm = jnp.sqrt(jnp.sum(group_square))
    ceiling = max_rms[0] * jnp.sqrt(jnp.float32((V + CAT) * D))
    factor = ceiling / (global_norm + 1e-06)
    head_output = (mtp_grad * factor).astype(jnp.bfloat16)
    embed_output = (lax.optimization_barrier(arrived).astype(jnp.float32) * factor).astype(
        jnp.bfloat16
    )
    return (embed_output, head_output, group_rms)


def solution(mesh):
    placed = (P("dp", "mp"), P("dp", "mp"), P(), P(), P())
    return jax.shard_map(
        on_device,
        mesh=mesh,
        in_specs=placed,
        out_specs=(P(("dp", "mp"), None), P("dp", "mp"), P()),
        check_vma=False,
    )
```

profile of v0, /device:TPU:0, one launch (start us, length us, event | category | flops | bytes accessed | tf_op | source)
XLA Modules:
  0.0 817.1 jit_solution(17026694794706699184)
XLA Ops:
  0.6 46.9 %multiply_reduce_fusion = (f32[16384]{0:T(1024)S(1)}, bf16[16384,896]{1,0:T(8,128)(2,1)}) fusion(f32[16384,896]{1,0:T(8,128)} %param.5), kind=kLoop, calls=%fused_computation.1 | loop fusion | flops 44023808 | bytes 88145920 | tf_op jit(solution)/shard_map/reduce_sum | solution.py:16
  47.5 0.0 copy-start
  47.5 0.0 copy-start.1
  47.5 7.4 all-to-all-start
  54.9 5.6 multiply_reduce_fusion.1
  60.5 0.1 reduce_sum.82
  60.6 0.1 reduce_sum.83
  60.7 0.1 reduce_sum.79
  60.8 0.0 copy-done
  60.8 0.1 dynamic_slice.6
  60.9 0.0 copy-done.1
  60.9 0.1 dynamic_slice.7
  61.0 0.1 select_reduce_fusion.1
  61.1 0.1 select_reduce_fusion
  61.2 647.7 %psum.7 = f32[32]{0:T(128)S(1)} all-reduce(f32[32]{0:T(128)S(1)} %add.19), channel_id=1, replica_groups=mesh['dp'=4,'mp'=8] {'dp','mp'}, use_global_device_ids=true, to_apply=%region_6.0 | all-reduce | flops 32 | bytes 256 | tf_op jit(solution)/shard_map/psum | solution.py:37
  709.5 0.1 convert_reduce_fusion.1
  709.6 0.1 convert_reduce_fusion
  709.7 1.1 fusion
  711.6 8.4 %multiply_convert_fusion.1 = bf16[3584,896]{1,0:T(8,128)(2,1)} fusion(f32[3584,896]{1,0:T(8,128)} %param.6, f32[]{:T(128)S(6)} %div.6), kind=kLoop, calls=%fused_computation.2 | loop fusion | flops 6422528 | bytes 19267588 | tf_op jit(solution)/shard_map/convert_element_type | solution.py:45
  720.0 0.0 all-to-all-done
  720.0 40.7 %copy.11 = bf16[8,2048,896]{1,2,0:T(8,128)(2,1)} copy(bf16[8,2048,896]{2,1,0:T(8,128)(2,1)} %all-to-all-done) | data formatting | bytes 58720256 | tf_op jit(solution)/shard_map/all_to_all | solution.py:30
  760.7 20.3 %multiply_convert_fusion = bf16[2048,7168]{0,1:T(8,128)(2,1)} fusion(bf16[2048,7168]{0,1:T(8,128)(2,1)} %bitcast.5, f32[]{:T(128)S(6)} %div.6), kind=kLoop, calls=%fused_computation | loop fusion | flops 44040192 | bytes 58720260 | tf_op jit(solution)/shard_map/convert_element_type | solution.py:46
  780.9 36.2 %copy.12 = bf16[2048,7168]{1,0:T(8,128)(2,1)} copy(bf16[2048,7168]{0,1:T(8,128)(2,1)} %multiply_convert_fusion) | data formatting | bytes 58720256
  (2 shorter events, 0.0 us)
Async XLA Ops:
  47.5 13.3 %copy-start = (s32[64]{0:T(128)S(1)}, s32[64]{0:T(128)}, u32[]{:S(2)}) copy-start(s32[64]{0:T(128)} %param.7) | copy-start | bytes 772
  47.5 13.4 %copy-start.1 = (s32[32]{0:T(128)S(1)}, s32[32]{0:T(128)}, u32[]{:S(2)}) copy-start(s32[32]{0:T(128)} %param.8) | copy-start | bytes 388
  47.5 672.5 %all-to-all-start = ((bf16[8,2048,896]{2,1,0:T(8,128)(2,1)}), bf16[8,2048,896]{2,1,0:T(8,128)(2,1)}, u32[]{:S(2)}, u32[]{:S(2)}) async-start(bf16[8,2048,896]{2,1,0:T(8,128)(2,1)} %bitcast.6), calls=%async_computation | async-start | bytes 58720256 | tf_op jit(solution)/shard_map/all_to_all | solution.py:30
where the time goes:
time: 819 us; the launch traced here: 817 us
  blocking collectives  648 us (79%)
  other arithmetic  82.8 us (10%)
  local copies, waits for them, and re-layouts  77.2 us (9%)
    psum x1, blocking collectives, on_device(): group_square = lax.psum(partial_value, ('dp', 'mp'))  648 us
    reduce_sum x4, other arithmetic, block_squares(): return jnp.sum(jnp.square(blocks), axis=(1, 2))  52.7 us
    all_to_all x1, local copies, waits for them, and re-layouts, on_device(): lax.all_to_all(emb_low, 'mp', split_axis=0, concat_axis=1, tiled=True)  40.7 us
    unnamed x5, local copies, waits for them, and re-layouts  36.2 us
    convert_element_type x1, other arithmetic, on_device(): (lax.optimization_barrier(arrived).astype(jnp.float32) * factor).astype(j...  20.3 us
  transfers between devices with their start and end apart: 1, of which 0 were waited for; matrix products, arithmetic and copies ran while one was open for 2% of the time, Pallas kernels for 0%

commit v1 on v0

--- a/solution.py
+++ b/solution.py
@@ -2,6 +2,7 @@
 import jax.numpy as jnp
 from jax import lax
 from jax.sharding import PartitionSpec as P
+from jax.lax import all_to_all, axis_size
 
 D = 7168
 V = 65536
@@ -27,7 +28,9 @@
     embed_labels = lax.dynamic_slice_in_dim(emb_groups, shard * embed_count, embed_count)
     head_labels = lax.dynamic_slice_in_dim(mtp_groups, shard * head_count, head_count)
     emb_low = lax.optimization_barrier(emb_grad.astype(jnp.bfloat16))
-    arrived = lax.all_to_all(emb_low, "mp", split_axis=0, concat_axis=1, tiled=True)
+    arrived = jnp.concatenate(
+        all_to_all(jnp.stack(jnp.split(emb_low, axis_size("mp"), 0), 0), "mp", 0, 0), 1
+    )
     partial_value = jnp.sum(
         block_squares(emb_grad, EMB_BLK)[:, None] * membership(embed_labels), axis=0
     )

time: 819 us -> 789 us (0.963)
  local copies, waits for them, and re-layouts: 77.2 us -> 48.5 us
    all_to_all x1 -> x0, local copies, waits for them, and re-layouts: 40.7 us -> none  [on_device(): lax.all_to_all(emb_low, 'mp', split_axis=0, concat_axis=1, tiled=True)]
    reshape x0 -> x1, local copies, waits for them, and re-layouts: none -> 20.5 us  [on_device(): jnp.concatenate(all_to_all(jnp.stack(jnp.split(emb_low, axis_size('mp'),...]
    unnamed x5 -> x13, local copies, waits for them, and re-layouts: 36.2 us -> 25.7 us
where the time goes in v1:
time: 789 us
  blocking collectives  648 us (82%)
  other arithmetic  83 us (11%)
  local copies, waits for them, and re-layouts  48.5 us (6%)
    psum x1, blocking collectives, on_device(): group_square = lax.psum(partial_value, ('dp', 'mp'))  648 us
    reduce_sum x4, other arithmetic, block_squares(): return jnp.sum(jnp.square(blocks), axis=(1, 2))  52.7 us
    unnamed x13, local copies, waits for them, and re-layouts  25.7 us
    reshape x1, local copies, waits for them, and re-layouts, on_device(): jnp.concatenate(all_to_all(jnp.stack(jnp.split(emb_low, axis_size('mp'),...  20.5 us
    convert_element_type x1, other arithmetic, on_device(): (lax.optimization_barrier(arrived).astype(jnp.float32) * factor).astype(j...  20.4 us
  transfers between devices with their start and end apart: 1, of which 0 were waited for; matrix products, arithmetic and copies ran while one was open for 2% of the time, Pallas kernels for 0%

profile of v1, /device:TPU:0, one launch (start us, length us, event | category | flops | bytes accessed | tf_op | source)
XLA Modules:
  0.0 788.6 jit_solution(7474511711609141693)
XLA Ops:
  0.6 46.9 %multiply_reduce_fusion = (f32[16384]{0:T(1024)S(1)}, bf16[16384,896]{1,0:T(8,128)(2,1)}) fusion(f32[16384,896]{1,0:T(8,128)} %param.5), kind=kLoop, calls=%fused_computation.1 | loop fusion | flops 44023808 | bytes 88145920 | tf_op jit(solution)/shard_map/reduce_sum | solution.py:17
  47.5 4.3 fusion.7
  51.8 5.0 fusion.6
  56.8 5.0 fusion.5
  61.8 4.9 fusion.4
  66.7 2.2 fusion.3
  68.9 2.1 fusion.2
  71.0 2.2 fusion.1
  73.2 2.1 fusion
  75.3 7.4 all-to-all-start
  82.7 5.6 multiply_reduce_fusion.1
  88.3 0.1 reduce_sum.82
  88.3 0.1 reduce_sum.79
  88.5 0.1 reduce_sum.83
  88.6 0.1 dynamic_slice.6
  88.7 0.1 select_reduce_fusion
  88.8 0.1 select_reduce_fusion.1
  88.9 647.7 %psum.7 = f32[32]{0:T(128)S(1)} all-reduce(f32[32]{0:T(128)S(1)} %add.19), channel_id=1, replica_groups=mesh['dp'=4,'mp'=8] {'dp','mp'}, use_global_device_ids=true, to_apply=%region_6.0 | all-reduce | flops 32 | bytes 256 | tf_op jit(solution)/shard_map/psum | solution.py:40
  736.6 0.1 convert_reduce_fusion.1
  736.7 0.1 convert_reduce_fusion
  736.8 1.1 fusion.8
  739.3 8.4 %multiply_convert_fusion.1 = bf16[3584,896]{1,0:T(8,128)(2,1)} fusion(f32[3584,896]{1,0:T(8,128)} %param.6, f32[]{:T(128)S(6)} %div.6), kind=kLoop, calls=%fused_computation.2 | loop fusion | flops 6422528 | bytes 19267588 | tf_op jit(solution)/shard_map/convert_element_type | solution.py:48
  747.7 20.5 %copy.10 = bf16[8,256,8,896]{3,2,0,1:T(8,128)(2,1)} copy(bf16[8,256,8,896]{3,2,1,0:T(8,128)(2,1)} %bitcast.10) | data formatting | bytes 58720256 | tf_op jit(solution)/shard_map/reshape | solution.py:31
  768.2 20.4 %multiply_convert_fusion = bf16[2048,7168]{1,0:T(8,128)(2,1)} fusion(bf16[2048,7168]{1,0:T(8,128)(2,1)} %bitcast.36, f32[]{:T(128)S(6)} %div.6), kind=kLoop, calls=%fused_computation | loop fusion | flops 44040192 | bytes 58720260 | tf_op jit(solution)/shard_map/convert_element_type | solution.py:49
  (10 shorter events, 0.1 us)
Async XLA Ops:
  47.5 19.2 %copy-start = (bf16[16384,896]{1,0:T(8,128)(2,1)S(1)}, bf16[16384,896]{1,0:T(8,128)(2,1)}, u32[]{:S(2)}) copy-start(bf16[16384,896]{1,0:T(8,128)(2,1)} %get-tuple-element.4) | copy-start | bytes 88080384
  75.3 13.3 %copy-start.1 = (s32[64]{0:T(128)S(1)}, s32[64]{0:T(128)}, u32[]{:S(2)}) copy-start(s32[64]{0:T(128)} %param.7) | copy-start | bytes 772
  75.3 13.4 %copy-start.2 = (s32[32]{0:T(128)S(1)}, s32[32]{0:T(128)}, u32[]{:S(2)}) copy-start(s32[32]{0:T(128)} %param.8) | copy-start | bytes 388
  75.3 672.4 %all-to-all-start = ((bf16[8,2048,896]{2,1,0:T(8,128)(2,1)}), bf16[8,2048,896]{2,1,0:T(8,128)(2,1)}, u32[]{:S(2)}, u32[]{:S(2)}) async-start(bf16[8,2048,896]{2,1,0:T(8,128)(2,1)} %fusion), calls=%async_computation | async-start | bytes 58720256 | tf_op jit(solution)/shard_map/all_to_all | solution.py:32

commit v2 on v0

--- a/solution.py
+++ b/solution.py
@@ -9,6 +9,12 @@
 EMB_BLK = 1024
 MTP_BLK = 448
 GROUPS = 32
+
+
+def gather_and_add(x, name):
+    pieces = lax.all_gather(x, name, axis=0, tiled=False)
+    acc = pieces.sum(axis=0)
+    return acc
 
 
 def block_squares(gradient, block_rows):
@@ -34,7 +40,7 @@
     partial_value = partial_value + jnp.sum(
         block_squares(mtp_grad, MTP_BLK)[:, None] * membership(head_labels), axis=0
     )
-    group_square = lax.psum(partial_value, ("dp", "mp"))
+    group_square = gather_and_add(partial_value, ("dp", "mp"))
     group_size = jnp.sum(membership(emb_groups), axis=0) * jnp.float32(EMB_BLK * D) + jnp.sum(
         membership(mtp_groups), axis=0
     ) * jnp.float32(MTP_BLK * D)

time: 819 us -> 819 us (level)
    psum x1 -> x0, blocking collectives: 648 us -> none  [on_device(): group_square = lax.psum(partial_value, ('dp', 'mp'))]
    unnamed x0 -> x1, blocking collectives: none -> 648 us
    unnamed x5 -> x6, local copies, waits for them, and re-layouts: 36.2 us -> 36.2 us
where the time goes in v2:
time: 819 us; the launch traced here: 817 us
  blocking collectives  648 us (79%)
  other arithmetic  83 us (10%)
  local copies, waits for them, and re-layouts  77.2 us (9%)
    unnamed x1, blocking collectives  648 us
    reduce_sum x4, other arithmetic, block_squares(): return jnp.sum(jnp.square(blocks), axis=(1, 2))  52.7 us
    all_to_all x1, local copies, waits for them, and re-layouts, on_device(): lax.all_to_all(emb_low, 'mp', split_axis=0, concat_axis=1, tiled=True)  40.7 us
    unnamed x6, local copies, waits for them, and re-layouts  36.2 us
    convert_element_type x1, other arithmetic, on_device(): (lax.optimization_barrier(arrived).astype(jnp.float32) * factor).astype(j...  20.3 us
  transfers between devices with their start and end apart: 1, of which 0 were waited for; matrix products, arithmetic and copies ran while one was open for 2% of the time, Pallas kernels for 0%

profile of v2, /device:TPU:0, one launch (start us, length us, event | category | flops | bytes accessed | tf_op | source)
XLA Modules:
  0.0 817.2 jit_solution(12320240977675056123)
XLA Ops:
  0.6 46.9 %multiply_reduce_fusion = (f32[16384]{0:T(1024)S(1)}, bf16[16384,896]{1,0:T(8,128)(2,1)}) fusion(f32[16384,896]{1,0:T(8,128)} %param.5), kind=kLoop, calls=%fused_computation.1 | loop fusion | flops 44023808 | bytes 88145920 | tf_op jit(solution)/shard_map/reduce_sum | solution.py:22
  47.5 7.4 all-to-all-start
  54.9 5.6 multiply_reduce_fusion.1
  60.5 0.1 reduce_sum.91
  60.6 0.1 reduce_sum.88
  60.7 0.1 reduce_sum.92
  60.8 0.0 copy-done
  60.8 0.1 dynamic_slice.6
  60.9 0.0 copy-done.1
  60.9 0.1 dynamic_slice.7
  61.0 0.1 select_reduce_fusion
  61.1 0.1 select_reduce_fusion.1
  61.2 0.1 add_dynamic-update-slice_fusion
  61.3 647.6 %all-reduce = f32[1024]{0:T(1024)S(1)} all-reduce(f32[1024]{0:T(1024)S(1)} %add_dynamic-update-slice_fusion), channel_id=2, replica_groups=mesh['dp'=4,'mp'=8] {'dp','mp'}, use_global_device_ids=true, to_apply=%add | all-reduce | flops 1024 | bytes 8192
  708.8 0.6 reduce_sum.94
  709.4 0.1 reshape.33
  710.9 0.1 convert_reduce_fusion.1
  711.0 0.1 convert_reduce_fusion
  711.1 0.5 fusion
  711.7 8.4 %multiply_convert_fusion.1 = bf16[3584,896]{1,0:T(8,128)(2,1)} fusion(f32[3584,896]{1,0:T(8,128)} %param.6, f32[]{:T(128)S(6)} %div.6), kind=kLoop, calls=%fused_computation.2 | loop fusion | flops 6422528 | bytes 19267588 | tf_op jit(solution)/shard_map/convert_element_type | solution.py:51
  720.1 0.0 all-to-all-done
  720.1 40.7 %copy.11 = bf16[8,2048,896]{1,2,0:T(8,128)(2,1)} copy(bf16[8,2048,896]{2,1,0:T(8,128)(2,1)} %all-to-all-done) | data formatting | bytes 58720256 | tf_op jit(solution)/shard_map/all_to_all | solution.py:36
  760.8 20.3 %multiply_convert_fusion = bf16[2048,7168]{0,1:T(8,128)(2,1)} fusion(bf16[2048,7168]{0,1:T(8,128)(2,1)} %bitcast.5, f32[]{:T(128)S(6)} %div.6), kind=kLoop, calls=%fused_computation | loop fusion | flops 44040192 | bytes 58720260 | tf_op jit(solution)/shard_map/convert_element_type | solution.py:52
  781.0 36.2 %copy.12 = bf16[2048,7168]{1,0:T(8,128)(2,1)} copy(bf16[2048,7168]{0,1:T(8,128)(2,1)} %multiply_convert_fusion) | data formatting | bytes 58720256
  (5 shorter events, 0.0 us)
Async XLA Ops:
  47.5 13.3 %copy-start = (s32[64]{0:T(128)S(1)}, s32[64]{0:T(128)}, u32[]{:S(2)}) copy-start(s32[64]{0:T(128)} %param.7) | copy-start | bytes 772
  47.5 13.4 %copy-start.1 = (s32[32]{0:T(128)S(1)}, s32[32]{0:T(128)}, u32[]{:S(2)}) copy-start(s32[32]{0:T(128)} %param.8) | copy-start | bytes 388
  47.5 672.6 %all-to-all-start = ((bf16[8,2048,896]{2,1,0:T(8,128)(2,1)}), bf16[8,2048,896]{2,1,0:T(8,128)(2,1)}, u32[]{:S(2)}, u32[]{:S(2)}) async-start(bf16[8,2048,896]{2,1,0:T(8,128)(2,1)} %bitcast.6), calls=%async_computation | async-start | bytes 58720256 | tf_op jit(solution)/shard_map/all_to_all | solution.py:36
